TPU v7x, 32 devices: a whole 2x2x4 slice. The times are simulated.
32 devices in a mesh: dp: 4 (over x, core), tensor: 8 (over z, y).
Axes of the slice: x: 2, y: 2, z: 4, core: 2. Of those that a mesh axis runs over, the one named last changes fastest.
Arguments:
- attn_out: bfloat16 [96, 8192], P('dp', 'tensor'), parts along dimension 0, may hold values from -6 to 6
- w_out: bfloat16 [8192, 7168], P('tensor'), may hold values from -0.0625 to 0.0625
- residual: bfloat16 [96, 7168], P(('dp', 'tensor')), parts along dimension 0, may hold values from -6 to 6
- norm_gain: float32 [7168], replicated, may hold values from 0.1 to 1.9
Outputs:
- new_stream: bfloat16 [96, 7168], P(('dp', 'tensor')), parts along dimension 0
- quantized: bfloat16 [96, 7168], P(('dp', 'tensor')), parts along dimension 0
- block_scales: float32 [96, 56], P(('dp', 'tensor')), parts along dimension 0
There are 4 independent parts, one for each index of `dp`. A program takes and returns all parts, laid end to end along the dimension named above; an argument that names none is the same for every part. Nothing has to cross between parts.
All inputs are finite; a program needn't handle non-finite values. Where the computation divides by a largest or mean magnitude, that divisor is 1e-20 or more.
Results may differ from a plain program's by a relative error of at most 0.0014.
Values sent between devices are 32-bit elements; how exact they have to be, the bound alone decides.
No kernel may reach another device: no remote copies, remote signals or barrier semaphores. Data moves between devices by JAX's collectives and lax.ppermute only.
A program may use at most 64 MiB of HBM per device.

v0:
```python
import jax
import jax.numpy as jnp
from jax import lax
from jax.sharding import PartitionSpec as P

BLOCK = 128


def finish(hidden, norm_gain, block_width):
    count = hidden.shape[0]
    width = hidden.shape[1]
    new_stream = hidden.astype(jnp.bfloat16)
    mean_square = jnp.mean(hidden * hidden, axis=1, keepdims=True)
    normed = hidden * lax.rsqrt(mean_square + 1e-06) * norm_gain
    blocks = normed.reshape(count, width // block_width, block_width)
    peak_abs = jnp.max(jnp.abs(blocks), axis=2) + 1e-06
    quantized = (blocks * 448.0 / peak_abs[:, :, None]).reshape(count, width).astype(jnp.bfloat16)
    return (new_stream, quantized, peak_abs / 448.0)


def local(attn_out, w_out, residual, norm_gain):
    groups = lax.axis_size("tensor")
    count = residual.shape[0]
    width = residual.shape[1]
    partial_value = jnp.dot(attn_out, w_out, preferred_element_type=jnp.float32)
    stacked = partial_value.reshape(groups, count, width)
    received = lax.all_to_all(stacked, "tensor", split_axis=0, concat_axis=0, tiled=True)
    mine = jnp.sum(received, axis=0)
    hidden = residual.astype(jnp.float32) + mine
    return finish(hidden, norm_gain, BLOCK)


def solution(mesh):
    return jax.shard_map(
        local,
        mesh=mesh,
        in_specs=(P("dp", "tensor"), P("tensor", None), P(("dp", "tensor"), None), P()),
        out_specs=(P(("dp", "tensor"), None), P(("dp", "tensor"), None), P(("dp", "tensor"), None)),
        check_vma=False,
    )
```

profile of v0, /device:TPU:0, one launch (start us, length us, event | category | flops | bytes accessed | tf_op | source)
XLA Modules:
  0.0 41.3 jit_solution(541114304981518494)
XLA Ops:
  0.6 0.0 copy-start
  0.6 0.0 copy-start.1
  0.7 0.8 %copy-done = bf16[24,1024]{1,0:T(8,128)(2,1)S(1)} copy-done((bf16[24,1024]{1,0:T(8,128)(2,1)S(1)}, bf16[24,1024]{1,0:T(8,128)(2,1)}, u32[]{:S(2)}) %copy-start) | copy-done | bytes 49176
  1.4 0.0 copy-start.2
  1.4 7.2 %fusion.2 = f32[24,7168]{1,0:T(8,128)S(1)} fusion(bf16[24,1024]{1,0:T(8,128)(2,1)S(1)} %copy-done, bf16[1024,7168]{1,0:T(8,128)(2,1)} %param.5), kind=kOutput, calls=%fused_computation.12 | convolution fusion | flops 352321536 | bytes 15417344 | tf_op jit(solution)/shard_map/dot_general | solution.py:25
  8.6 0.3 reshape.25
  8.9 30.4 %all_to_all.5 = f32[8,3,7168]{2,1,0:T(4,128)S(1)} all-to-all(f32[8,3,7168]{2,1,0:T(4,128)S(1)} %reshape.25), channel_id=1, replica_groups=mesh['dp'=4,'tensor'=8] {'tensor'}, dimensions={0} | all-to-all | bytes 1376256 | tf_op jit(solution)/shard_map/all_to_all | solution.py:27
  39.3 0.2 reduce_sum.18
  39.5 0.0 copy-done.1
  39.5 0.2 multiply_reduce_fusion
  39.7 0.0 copy-done.2
  39.7 0.1 abs_bitcast_fusion
  39.8 0.1 bitcast_reduce_fusion
  39.9 0.6 %broadcast_multiply_fusion = (f32[3,56]{1,0:T(4,128)}, f32[3,56]{1,0:T(4,128)S(1)}) fusion(f32[3,56]{1,0:T(4,128)S(1)} %bitcast_reduce_fusion), kind=kLoop, calls=%fused_computation.8 | loop fusion | flops 336 | bytes 2016 | tf_op jit(solution)/shard_map/div | solution.py:18
  40.5 0.1 broadcast_bitcast_fusion
  40.6 0.7 %fusion = (bf16[3,7168]{1,0:T(4,128)(2,1)}, bf16[3,7168]{1,0:T(4,128)(2,1)}) fusion(f32[1,3,56,128]{3,2,1,0:T(8,128)S(1)} %broadcast_bitcast_fusion, f32[7168]{0:T(1024)S(1)} %copy-done.2, f32[3]{0:T(128)S(1)} %add_rsqrt_fusion, f32[3,7168]{1,0:T(4,128)S(1)} %reduce_sum.18, bf16[3,7168]{1,0:T(4,128)(2,1)S(1)} %copy-done.1), kind=kLoop, calls=%fused_computation.5 | loop fusion | flops 172032 | bytes 329740 | tf_op jit(solution)/shard_map/convert_element_type | solution.py:17
  (1 shorter events, 0.0 us)
Async XLA Ops:
  0.6 0.8 %copy-start = (bf16[24,1024]{1,0:T(8,128)(2,1)S(1)}, bf16[24,1024]{1,0:T(8,128)(2,1)}, u32[]{:S(2)}) copy-start(bf16[24,1024]{1,0:T(8,128)(2,1)} %param.4) | copy-start | bytes 147460
  0.6 38.9 %copy-start.1 = (bf16[3,7168]{1,0:T(4,128)(2,1)S(1)}, bf16[3,7168]{1,0:T(4,128)(2,1)}, u32[]{:S(2)}) copy-start(bf16[3,7168]{1,0:T(4,128)(2,1)} %param.6) | copy-start | bytes 129028
  1.4 38.3 %copy-start.2 = (f32[7168]{0:T(1024)S(1)}, f32[7168]{0:T(1024)}, u32[]{:S(2)}) copy-start(f32[7168]{0:T(1024)} %param.7) | copy-start | bytes 86020
where the time goes:
time: 41.5 us; the launch traced here: 41.3 us
  blocking collectives  30.4 us (73%)
  matrix products  7.2 us (17%)
  other arithmetic  1.87 us (5%)
  local copies, waits for them, and re-layouts  1.17 us (3%)
  between operations  0.69 us (2%)
    all_to_all x1, blocking collectives, local(): lax.all_to_all(stacked, 'tensor', split_axis=0, concat_axis=0, tiled=True)  30.4 us
    dot_general x1, matrix products, local(): partial_value = jnp.dot(attn_out, w_out, preferred_element_type=jnp.float32)  7.2 us
    unnamed x7, local copies, waits for them, and re-layouts  0.87 us

commit v1 on v0

v1 whole, which is shorter than its diff:
```python
import functools
import jax
import jax.numpy as jnp
from jax import lax
from jax.experimental import pallas as pl
from jax.experimental.pallas import tpu as pltpu
from jax.sharding import PartitionSpec as P

BLOCK = 128
AXIS = "tensor"


def product_kernel(order, rows, strip, attn_ref, w_ref, out_ref, w_buf, sems):
    tokens = attn_ref.shape[0]
    width = w_ref.shape[1]
    blocks = width // BLOCK
    strips = width // strip
    copies = [
        pltpu.make_async_copy(
            w_ref.at[:, pl.ds(s * strip, strip)], w_buf.at[s], sems.at[s]
        )
        for s in range(strips)
    ]
    for copy in copies:
        copy.start()
    me = lax.axis_index(AXIS)
    pos = lax.broadcasted_iota(jnp.int32, (tokens, tokens), 0)
    col = lax.broadcasted_iota(jnp.int32, (tokens, tokens), 1)
    slot = pos // rows
    member = jnp.zeros_like(slot)
    for place, mask in enumerate(order):
        member = jnp.where(slot == place, mask, member)
    want = (member ^ me) * rows + (pos - slot * rows)
    pick = jnp.where(col == want, 1.0, 0.0).astype(jnp.bfloat16)
    mine = jnp.dot(pick, attn_ref[...], preferred_element_type=jnp.float32).astype(jnp.bfloat16)
    for s in range(strips):
        copies[s].wait()
        acc = jnp.dot(mine, w_buf[s], preferred_element_type=jnp.float32)
        for c in range(strip // BLOCK):
            out_ref[pl.ds(s * (strip // BLOCK) + c, tokens, stride=blocks), :] = acc[:, c * BLOCK : (c + 1) * BLOCK]


def product(attn, w, order, rows):
    tokens, depth = attn.shape
    width = w.shape[1]
    strip = 512 if width % 512 == 0 else BLOCK
    strips = width // strip
    return pl.pallas_call(
        functools.partial(product_kernel, order, rows, strip),
        out_shape=jax.ShapeDtypeStruct((tokens * width // BLOCK, BLOCK), jnp.float32),
        in_specs=[pl.BlockSpec(memory_space=pltpu.VMEM), pl.BlockSpec(memory_space=pl.ANY)],
        out_specs=pl.BlockSpec(memory_space=pltpu.VMEM),
        scratch_shapes=[
            pltpu.VMEM((strips, depth, strip), jnp.bfloat16),
            pltpu.SemaphoreType.DMA((strips,)),
        ],
        compiler_params=pltpu.CompilerParams(vmem_limit_bytes=40 * 1024 * 1024),
        cost_estimate=pl.CostEstimate(flops=2 * tokens * depth * width, bytes_accessed=2 * depth * width, transcendentals=0),
        name="product",
    )(attn, w)


def tail_kernel(rows, base_ref, got_ref, gain_ref, new_ref, quant_ref, scale_ref, hid, nrm):
    blocks = gain_ref.shape[0]
    for j in range(rows):
        at = pl.ds(j * blocks, blocks)
        hidden = base_ref[at, :] + got_ref[at, :]
        hid[at, :] = hidden
        total = jnp.sum(hidden * hidden, axis=(0, 1), keepdims=True)
        normed = hidden * lax.rsqrt(total / (blocks * BLOCK) + 1e-06) * gain_ref[...]
        peak = jnp.max(jnp.abs(normed), axis=1, keepdims=True) + 1e-06
        nrm[at, :] = normed * 448.0 / peak
        scale_ref[pl.ds(j, 1), :] = jnp.transpose(jnp.broadcast_to(peak / 448.0, (blocks, BLOCK)))[:1, :]
    for c in range(blocks):
        lanes = pl.ds(c * BLOCK, BLOCK)
        new_ref[:, lanes] = hid[pl.ds(c, rows, stride=blocks), :].astype(jnp.bfloat16)
        quant_ref[:, lanes] = nrm[pl.ds(c, rows, stride=blocks), :].astype(jnp.bfloat16)


def tail(base, got, gain, rows):
    blocks = gain.shape[0]
    width = blocks * BLOCK
    return pl.pallas_call(
        functools.partial(tail_kernel, rows),
        out_shape=(
            jax.ShapeDtypeStruct((rows, width), jnp.bfloat16),
            jax.ShapeDtypeStruct((rows, width), jnp.bfloat16),
            jax.ShapeDtypeStruct((rows, blocks), jnp.float32),
        ),
        in_specs=[pl.BlockSpec(memory_space=pltpu.VMEM)] * 3,
        out_specs=[pl.BlockSpec(memory_space=pltpu.VMEM)] * 3,
        scratch_shapes=[pltpu.VMEM((rows * blocks, BLOCK), jnp.float32)] * 2,
        name="tail",
    )(base, got, gain)


def local(attn_out, w_out, residual, norm_gain):
    groups = lax.axis_size(AXIS)
    rows, width = residual.shape
    blocks = width // BLOCK
    near = min(4, groups)
    far = groups // near
    order = [f * near + q for q in range(near) for f in range(far)]

    def swap(value, mask):
        return lax.ppermute(value, AXIS, [(i, i ^ mask) for i in range(groups)])

    buf = product(attn_out, w_out, order, rows)
    quarter = buf.shape[0] // near
    parts = [buf[q * quarter : (q + 1) * quarter] for q in range(near)]
    got = [swap(parts[q], q) for q in range(1, near)]
    mine = parts[0]
    for g in got:
        mine = mine + g
    base = residual.astype(jnp.float32).reshape(rows * blocks, BLOCK)
    mask = groups // 2
    last = jnp.zeros_like(base)
    while mask >= near:
        half = mine.shape[0] // 2
        last = swap(mine[half:], mask)
        mine = mine[:half]
        if mask > near:
            mine = mine + last
        mask //= 2
    return tail(base + mine, last, norm_gain.reshape(blocks, BLOCK), rows)


def solution(mesh):
    return jax.shard_map(
        local,
        mesh=mesh,
        in_specs=(P("dp", "tensor"), P("tensor", None), P(("dp", "tensor"), None), P()),
        out_specs=(P(("dp", "tensor"), None), P(("dp", "tensor"), None), P(("dp", "tensor"), None)),
        check_vma=False,
    )
```

time: 41.5 us -> 28.3 us (0.68)
  blocking collectives: 30.4 us -> 0 us
  waiting for transfers between devices: 0 us -> 10.3 us
  Pallas kernels: 0 us -> 7.56 us
  starting transfers between devices: 0 us -> 7.38 us
  matrix products: 7.2 us -> 0 us
  other arithmetic: 1.87 us -> 0.69 us
    all_to_all x1 -> x0, blocking collectives: 30.4 us -> none  [local(): lax.all_to_all(stacked, 'tensor', split_axis=0, concat_axis=0, tiled=True)]
    ppermute x0 -> x4, waiting for transfers between devices: none -> 10.3 us  [swap(): return lax.ppermute(value, AXIS, [(i, i ^ mask) for i in range(groups)])]
    pallas_call x0 -> x2, Pallas kernels: none -> 7.56 us  [the longest x1 5.73 us: product(): pl.pallas_call(functools.partial(product_kernel, order, rows, strip), out...]
    ppermute x0 -> x4, starting transfers between devices: none -> 7.38 us  [swap(): return lax.ppermute(value, AXIS, [(i, i ^ mask) for i in range(groups)])]
    dot_general x1 -> x0, matrix products: 7.2 us -> none  [local(): partial_value = jnp.dot(attn_out, w_out, preferred_element_type=jnp.float32)]
    convert_element_type x1 -> x0, other arithmetic: 0.74 us -> none  [finish(): (blocks * 448.0 / peak_abs[:, :, None]).reshape(count, width)]
    slice x0 -> x1, other arithmetic: none -> 0.65 us  [local(): last = swap(mine[half:], mask)]
    div x1 -> x0, other arithmetic: 0.59 us -> none  [finish(): return (new_stream, quantized, peak_abs / 448.0)]
  transfers between devices with their start and end apart: 0 -> 4, of which waited for: 0 -> 4; matrix products, arithmetic and copies ran while one was open for 0% -> 0% of each run, Pallas kernels for 0% -> 0%
where the time goes in v1:
time: 28.3 us; the launch traced here: 28.1 us
  waiting for transfers between devices  10.3 us (36%)
  Pallas kernels  7.56 us (27%)
  starting transfers between devices  7.38 us (26%)
  local copies, waits for them, and re-layouts  1.49 us (5%)
  other arithmetic  0.69 us (2%)
  between operations  0.67 us (2%)
    ppermute x4, waiting for transfers between devices, swap(): return lax.ppermute(value, AXIS, [(i, i ^ mask) for i in range(groups)])  10.3 us
    ppermute x4, starting transfers between devices, swap(): return lax.ppermute(value, AXIS, [(i, i ^ mask) for i in range(groups)])  7.38 us
    pallas_call x1, Pallas kernels, product(): pl.pallas_call(functools.partial(product_kernel, order, rows, strip), out...  5.73 us
    pallas_call x1, Pallas kernels, tail(): pl.pallas_call(functools.partial(tail_kernel, rows), out_shape=(jax.Shape...  1.83 us
    unnamed x6, local copies, waits for them, and re-layouts  1.42 us
    slice x1, other arithmetic, local(): last = swap(mine[half:], mask)  0.65 us
  transfers between devices with their start and end apart: 4, of which 4 were waited for; matrix products, arithmetic and copies ran while one was open for 0% of the time, Pallas kernels for 0%

profile of v1, /device:TPU:0, one launch (start us, length us, event | category | flops | bytes accessed | tf_op | source)
XLA Modules:
  0.0 28.1 jit_solution(6661792840716370758)
XLA Ops:
  0.6 0.0 copy-start
  0.6 0.8 %copy-done = bf16[24,1024]{1,0:T(8,128)(2,1)S(1)} copy-done((bf16[24,1024]{1,0:T(8,128)(2,1)S(1)}, bf16[24,1024]{1,0:T(8,128)(2,1)}, u32[]{:S(2)}) %copy-start) | copy-done | bytes 49176
  1.4 0.0 copy-start.2
  1.4 5.7 %product.1 = f32[1344,128]{1,0:T(8,128)S(1)} custom-call(bf16[24,1024]{1,0:T(8,128)(2,1)S(1)} %copy-done, bf16[1024,7168]{1,0:T(8,128)(2,1)} %w_ref.1), custom_call_target="tpu_custom_call" | custom-call | flops 352321536 | bytes 14680064 | tf_op jit(solution)/shard_map/product/pallas_call | solution.py:48
  7.2 3.1 %collective-permute-start = (f32[336,128]{1,0:T(8,128)S(1)}, f32[336,128]{1,0:T(8,128)S(1)}, u32[]{:S(2)}, u32[]{:S(2)}) collective-permute-start(f32[336,128]{1,0:T(8,128)S(1)} %get-tuple-element.3), channel_id=1, source_target_pairs={{0,1},{1,0},{2,3},{3,2},{4,5},{5,4},{6,7},{7,6},{8,9},{9,8},{10,11... | collective-permute-start | bytes 516104 | tf_op jit(solution)/shard_map/ppermute | solution.py:106
  10.3 1.6 %collective-permute-start.1 = (f32[336,128]{1,0:T(8,128)S(1)}, f32[336,128]{1,0:T(8,128)S(1)}, u32[]{:S(2)}, u32[]{:S(2)}) collective-permute-start(f32[336,128]{1,0:T(8,128)S(1)} %get-tuple-element.5), channel_id=1, source_target_pairs={{0,2},{1,3},{2,0},{3,1},{4,6},{5,7},{6,4},{7,5},{8,10},{9,11},{10,... | collective-permute-start | bytes 516104 | tf_op jit(solution)/shard_map/ppermute | solution.py:106
  11.8 0.0 collective-permute-start.2
  11.9 0.0 copy-done.2
  11.9 2.8 %collective-permute-done = f32[336,128]{1,0:T(8,128)S(1)} collective-permute-done((f32[336,128]{1,0:T(8,128)S(1)}, f32[336,128]{1,0:T(8,128)S(1)}, u32[]{:S(2)}, u32[]{:S(2)}) %collective-permute-start) | collective-permute-done | bytes 172064 | tf_op jit(solution)/shard_map/ppermute | solution.py:106
  14.6 2.9 %collective-permute-done.1 = f32[336,128]{1,0:T(8,128)S(1)} collective-permute-done((f32[336,128]{1,0:T(8,128)S(1)}, f32[336,128]{1,0:T(8,128)S(1)}, u32[]{:S(2)}, u32[]{:S(2)}) %collective-permute-start.1) | collective-permute-done | bytes 172064 | tf_op jit(solution)/shard_map/ppermute | solution.py:106
  17.5 2.1 %collective-permute-done.2 = f32[336,128]{1,0:T(8,128)S(1)} collective-permute-done((f32[336,128]{1,0:T(8,128)S(1)}, f32[336,128]{1,0:T(8,128)S(1)}, u32[]{:S(2)}, u32[]{:S(2)}) %collective-permute-start.2) | collective-permute-done | bytes 172064 | tf_op jit(solution)/shard_map/ppermute | solution.py:106
  19.6 0.6 %fusion.3 = (f32[168,128]{1,0:T(8,128)S(1)}, f32[168,128]{1,0:T(8,128)}) fusion(f32[336,128]{1,0:T(8,128)S(1)} %fusion.1, f32[168,128]{1,0:T(8,128)S(1)} %reshape.19), kind=kLoop, calls=%fused_computation.5 | loop fusion | flops 21504 | bytes 430080 | tf_op jit(solution)/shard_map/slice | solution.py:120
  20.3 2.7 %collective-permute-start.3 = (f32[168,128]{1,0:T(8,128)S(1)}, f32[168,128]{1,0:T(8,128)S(1)}, u32[]{:S(2)}, u32[]{:S(2)}) collective-permute-start(f32[168,128]{1,0:T(8,128)S(1)} %get-tuple-element.6), channel_id=1, source_target_pairs={{0,4},{1,5},{2,6},{3,7},{4,0},{5,1},{6,2},{7,3},{8,12},{9,13},{10,... | collective-permute-start | bytes 258056 | tf_op jit(solution)/shard_map/ppermute | solution.py:106
  23.0 2.6 %collective-permute-done.3.got_ref = f32[168,128]{1,0:T(8,128)S(1)} collective-permute-done((f32[168,128]{1,0:T(8,128)S(1)}, f32[168,128]{1,0:T(8,128)S(1)}, u32[]{:S(2)}, u32[]{:S(2)}) %collective-permute-start.3) | collective-permute-done | bytes 86048 | tf_op jit(solution)/shard_map/ppermute | solution.py:106
  25.7 0.0 copy-start.1
  25.7 0.6 %copy-done.1 = f32[168,128]{1,0:T(8,128)} copy-done((f32[168,128]{1,0:T(8,128)}, f32[168,128]{1,0:T(8,128)S(1)}, u32[]{:S(2)}) %copy-start.1) | copy-done | bytes 86040
  26.3 1.8 %tail.1 = (bf16[3,7168]{1,0:T(4,128)(2,1)}, bf16[3,7168]{1,0:T(4,128)(2,1)}, f32[3,56]{1,0:T(4,128)}) custom-call(f32[168,128]{1,0:T(8,128)} %get-tuple-element.7.base_ref, f32[168,128]{1,0:T(8,128)} %copy-done.1, f32[56,128]{1,0:T(8,128)} %bitcast.1), custom_call_target="tpu_custom_call" | custom-call | tf_op jit(solution)/shard_map/tail/pallas_call | solution.py:83
  (3 shorter events, 0.1 us)
Async XLA Ops:
  0.6 0.8 %copy-start = (bf16[24,1024]{1,0:T(8,128)(2,1)S(1)}, bf16[24,1024]{1,0:T(8,128)(2,1)}, u32[]{:S(2)}) copy-start(bf16[24,1024]{1,0:T(8,128)(2,1)} %attn_ref.1) | copy-start | bytes 147460
  1.4 10.4 %copy-start.2 = (bf16[3,7168]{1,0:T(4,128)(2,1)S(1)}, bf16[3,7168]{1,0:T(4,128)(2,1)}, u32[]{:S(2)}) copy-start(bf16[3,7168]{1,0:T(4,128)(2,1)} %param.6) | copy-start | bytes 129028
  7.2 7.4 %collective-permute-start = (f32[336,128]{1,0:T(8,128)S(1)}, f32[336,128]{1,0:T(8,128)S(1)}, u32[]{:S(2)}, u32[]{:S(2)}) collective-permute-start(f32[336,128]{1,0:T(8,128)S(1)} %get-tuple-element.3), channel_id=1, source_target_pairs={{0,1},{1,0},{2,3},{3,2},{4,5},{5,4},{6,7},{7,6},{8,9},{9,8},{10,11... | collective-permute-start | bytes 516104 | tf_op jit(solution)/shard_map/ppermute | solution.py:106
  10.3 7.2 %collective-permute-start.1 = (f32[336,128]{1,0:T(8,128)S(1)}, f32[336,128]{1,0:T(8,128)S(1)}, u32[]{:S(2)}, u32[]{:S(2)}) collective-permute-start(f32[336,128]{1,0:T(8,128)S(1)} %get-tuple-element.5), channel_id=1, source_target_pairs={{0,2},{1,3},{2,0},{3,1},{4,6},{5,7},{6,4},{7,5},{8,10},{9,11},{10,... | collective-permute-start | bytes 516104 | tf_op jit(solution)/shard_map/ppermute | solution.py:106
  11.8 7.7 %collective-permute-start.2 = (f32[336,128]{1,0:T(8,128)S(1)}, f32[336,128]{1,0:T(8,128)S(1)}, u32[]{:S(2)}, u32[]{:S(2)}) collective-permute-start(f32[336,128]{1,0:T(8,128)S(1)} %get-tuple-element.4), channel_id=1, source_target_pairs={{0,3},{1,2},{2,1},{3,0},{4,7},{5,6},{6,5},{7,4},{8,11},{9,10},{10,... | collective-permute-start | bytes 516104 | tf_op jit(solution)/shard_map/ppermute | solution.py:106
  20.3 5.4 %collective-permute-start.3 = (f32[168,128]{1,0:T(8,128)S(1)}, f32[168,128]{1,0:T(8,128)S(1)}, u32[]{:S(2)}, u32[]{:S(2)}) collective-permute-start(f32[168,128]{1,0:T(8,128)S(1)} %get-tuple-element.6), channel_id=1, source_target_pairs={{0,4},{1,5},{2,6},{3,7},{4,0},{5,1},{6,2},{7,3},{8,12},{9,13},{10,... | collective-permute-start | bytes 258056 | tf_op jit(solution)/shard_map/ppermute | solution.py:106
  25.7 0.6 %copy-start.1 = (f32[168,128]{1,0:T(8,128)}, f32[168,128]{1,0:T(8,128)S(1)}, u32[]{:S(2)}) copy-start(f32[168,128]{1,0:T(8,128)S(1)} %collective-permute-done.3.got_ref) | copy-start | bytes 258052

commit v2 on v1

v2 whole, which is shorter than its diff:
```python
import functools
import jax
import jax.numpy as jnp
from jax import lax
from jax.experimental import pallas as pl
from jax.experimental.pallas import tpu as pltpu
from jax.sharding import PartitionSpec as P

BLOCK = 128
AXIS = "tensor"
MIB = 1024 * 1024


def up(value, step):
    return -(-value // step) * step


def product_kernel(order, rows, first, strip, attn_hbm, w_ref, *refs):
    near = len(order)
    outs, (attn_ref, w_buf, sems, attn_sem) = refs[:near], refs[near:]
    tokens = attn_ref.shape[0]
    held = tokens // near
    lot = up(held, 8)
    blocks = outs[0].shape[0] // held
    strips = blocks // strip
    fetch = pltpu.make_async_copy(attn_hbm, attn_ref, attn_sem)
    fetch.start()
    copies = [
        pltpu.make_async_copy(
            w_ref.at[:, pl.ds((first + s * strip) * BLOCK, strip * BLOCK)], w_buf.at[s], sems.at[s]
        )
        for s in range(strips)
    ]
    for copy in copies:
        copy.start()
    me = lax.axis_index(AXIS)
    pos = lax.broadcasted_iota(jnp.int32, (lot * near, tokens), 0)
    col = lax.broadcasted_iota(jnp.int32, (lot * near, tokens), 1)
    want = jnp.full_like(pos, -1)
    for q, masks in enumerate(order):
        for f, mask in enumerate(masks):
            start = q * lot + f * rows
            here = (pos >= start) & (pos < start + rows)
            want = jnp.where(here, (me ^ mask) * rows + pos - start, want)
    pick = jnp.where(col == want, 1.0, 0.0).astype(jnp.bfloat16)
    fetch.wait()
    mine = jnp.dot(pick, attn_ref[...], preferred_element_type=jnp.float32).astype(jnp.bfloat16)
    for s in range(strips):
        copies[s].wait()
        acc = jnp.dot(mine, w_buf[s], preferred_element_type=jnp.float32)
        for c in range(strip):
            for q in range(near):
                outs[q][pl.ds(s * strip + c, held, stride=blocks), :] = acc[
                    q * lot : q * lot + held, c * BLOCK : (c + 1) * BLOCK
                ]


def product(attn, w, order, rows, first, blocks):
    tokens, depth = attn.shape
    near = len(order)
    strip = next(s for s in (4, 2, 1) if blocks % s == 0)
    part = jax.ShapeDtypeStruct((tokens // near * blocks, BLOCK), jnp.float32)
    return pl.pallas_call(
        functools.partial(product_kernel, order, rows, first, strip),
        out_shape=[part] * near,
        in_specs=[pl.BlockSpec(memory_space=pl.ANY)] * 2,
        out_specs=[pl.BlockSpec(memory_space=pltpu.VMEM)] * near,
        scratch_shapes=[
            pltpu.VMEM((tokens, depth), jnp.bfloat16),
            pltpu.VMEM((blocks // strip, depth, strip * BLOCK), jnp.bfloat16),
            pltpu.SemaphoreType.DMA((blocks // strip,)),
            pltpu.SemaphoreType.DMA,
        ],
        compiler_params=pltpu.CompilerParams(vmem_limit_bytes=40 * MIB),
        cost_estimate=pl.CostEstimate(
            flops=2 * tokens * depth * blocks * BLOCK, bytes_accessed=2 * depth * blocks * BLOCK, transcendentals=0
        ),
        name="product",
    )(attn, w)


def fold_kernel(near, widths, rows, *refs):
    ins, (keep_ref, send_ref) = refs[:-2], refs[-2:]
    total = sum(widths)
    at = 0
    for k, blocks in enumerate(widths):
        group = ins[k * near : (k + 1) * near]
        slots = group[0].shape[0] // blocks
        for t in range(slots):
            lines = pl.ds(t * blocks, blocks)
            value = group[0][lines, :]
            for ref in group[1:]:
                value = value + ref[lines, :]
            out, spot = (keep_ref, t) if t < slots // 2 else (send_ref, t - slots // 2)
            out[pl.ds(spot * total + at, blocks), :] = value
        at += blocks


def fold(groups, widths, rows):
    near = len(groups[0])
    lines = sum(g[0].shape[0] for g in groups) // 2
    part = jax.ShapeDtypeStruct((lines, BLOCK), jnp.float32)
    return pl.pallas_call(
        functools.partial(fold_kernel, near, widths, rows),
        out_shape=[part] * 2,
        in_specs=[pl.BlockSpec(memory_space=pltpu.VMEM)] * (near * len(groups)),
        out_specs=[pl.BlockSpec(memory_space=pltpu.VMEM)] * 2,
        compiler_params=pltpu.CompilerParams(vmem_limit_bytes=12 * MIB),
        name="fold",
    )(*[value for group in groups for value in group])


def tail_kernel(rows, keep_ref, res_ref, gain_ref, got_ref, new_ref, quant_ref, scale_ref, hid, nrm):
    blocks = gain_ref.shape[0]
    line = lax.broadcasted_iota(jnp.int32, (blocks, BLOCK), 0)
    lane = lax.broadcasted_iota(jnp.int32, (blocks, BLOCK), 1)
    for j in range(rows):
        at = pl.ds(j * blocks, blocks)
        hidden = keep_ref[at, :] + got_ref[at, :] + res_ref[at, :]
        hid[at, :] = hidden
        square = jnp.sum(jnp.sum(hidden * hidden, axis=0, keepdims=True), axis=1, keepdims=True)
        normed = hidden * lax.rsqrt(square / (blocks * BLOCK) + 1e-06) * gain_ref[...]
        peak = jnp.max(jnp.abs(normed), axis=1, keepdims=True) + 1e-06
        nrm[at, :] = normed * 448.0 / peak
        spread = jnp.where(line == lane, peak / 448.0, 0.0)
        scale_ref[pl.ds(j, 1), :] = jnp.sum(spread, axis=0, keepdims=True)[:, :blocks]
    for c in range(blocks):
        lanes = pl.ds(c * BLOCK, BLOCK)
        new_ref[:, lanes] = hid[pl.ds(c, rows, stride=blocks), :].astype(jnp.bfloat16)
        quant_ref[:, lanes] = nrm[pl.ds(c, rows, stride=blocks), :].astype(jnp.bfloat16)


def tail(keep, res, gain, got, rows):
    blocks = gain.shape[0]
    width = blocks * BLOCK
    return pl.pallas_call(
        functools.partial(tail_kernel, rows),
        out_shape=(
            jax.ShapeDtypeStruct((rows, width), jnp.bfloat16),
            jax.ShapeDtypeStruct((rows, width), jnp.bfloat16),
            jax.ShapeDtypeStruct((rows, blocks), jnp.float32),
        ),
        in_specs=[pl.BlockSpec(memory_space=pltpu.VMEM)] * 4,
        out_specs=[pl.BlockSpec(memory_space=pltpu.VMEM)] * 3,
        scratch_shapes=[pltpu.VMEM((rows * blocks, BLOCK), jnp.float32)] * 2,
        compiler_params=pltpu.CompilerParams(vmem_limit_bytes=8 * MIB),
        name="tail",
    )(keep, res, gain, got)


def local(attn_out, w_out, residual, norm_gain):
    groups = lax.axis_size(AXIS)
    rows, width = residual.shape
    blocks = width // BLOCK
    near = min(4, groups // 2)
    order = [[f * near + q for f in range(groups // near)] for q in range(near)]

    def swap(value, mask):
        return lax.ppermute(value, AXIS, [(i, i ^ mask) for i in range(groups)])

    widths = [blocks]
    collected = []
    first = 0
    for wide in widths:
        parts = product(attn_out, w_out, order, rows, first, wide)
        collected.append([parts[0]] + [swap(parts[q], q) for q in range(1, near)])
        first += wide
    keep, send = fold(collected, widths, rows)

    mask = groups // 2
    while mask > near:
        half = keep.shape[0] // 2
        moved = swap(send, mask)
        keep, send = keep[:half] + moved[:half], keep[half:] + moved[half:]
        mask //= 2
    res = residual.astype(jnp.float32).reshape(rows * blocks, BLOCK)
    return tail(keep, res, norm_gain.reshape(blocks, BLOCK), swap(send, mask), rows)


def solution(mesh):
    return jax.shard_map(
        local,
        mesh=mesh,
        in_specs=(P("dp", "tensor"), P("tensor", None), P(("dp", "tensor"), None), P()),
        out_specs=(P(("dp", "tensor"), None), P(("dp", "tensor"), None), P(("dp", "tensor"), None)),
        check_vma=False,
    )
```

time: 28.3 us -> 26.1 us (0.922)
  Pallas kernels: 7.56 us -> 6.68 us
  other arithmetic: 0.69 us -> 0 us
  local copies, waits for them, and re-layouts: 1.49 us -> 0.83 us
    pallas_call x1, Pallas kernels: 1.83 us -> 0.87 us  [tail(): pl.pallas_call(functools.partial(tail_kernel, rows), out_shape=(jax.Shape...]
    slice x1 -> x0, other arithmetic: 0.65 us -> none  [local(): last = swap(mine[half:], mask)]
    unnamed x6, local copies, waits for them, and re-layouts: 1.42 us -> 0.8 us
    pallas_call x1 -> x2, Pallas kernels: 5.73 us -> 5.81 us  [the longest x1 5.77 us: product(): pl.pallas_call(functools.partial(product_kernel, order, rows, first, stri...]
where the time goes in v2:
time: 26.1 us; the launch traced here: 26 us
  waiting for transfers between devices  10.3 us (39%)
  starting transfers between devices  7.44 us (29%)
  Pallas kernels  6.68 us (26%)
  local copies, waits for them, and re-layouts  0.83 us (3%)
  between operations  0.66 us (3%)
    ppermute x4, waiting for transfers between devices, swap(): return lax.ppermute(value, AXIS, [(i, i ^ mask) for i in range(groups)])  10.3 us
    ppermute x4, starting transfers between devices, swap(): return lax.ppermute(value, AXIS, [(i, i ^ mask) for i in range(groups)])  7.44 us
    pallas_call x1, Pallas kernels, product(): pl.pallas_call(functools.partial(product_kernel, order, rows, first, stri...  5.77 us
    pallas_call x1, Pallas kernels, tail(): pl.pallas_call(functools.partial(tail_kernel, rows), out_shape=(jax.Shape...  0.87 us
    unnamed x6, local copies, waits for them, and re-layouts  0.8 us
  transfers between devices with their start and end apart: 4, of which 4 were waited for; matrix products, arithmetic and copies ran while one was open for 0% of the time, Pallas kernels for 0%

profile of v2, /device:TPU:0, one launch (start us, length us, event | category | flops | bytes accessed | tf_op | source)
XLA Modules:
  0.0 26.0 jit_solution(15407466157817715519)
XLA Ops:
  0.6 0.0 copy-start
  0.6 0.8 %copy-done = bf16[24,1024]{1,0:T(8,128)(2,1)S(1)} copy-done((bf16[24,1024]{1,0:T(8,128)(2,1)S(1)}, bf16[24,1024]{1,0:T(8,128)(2,1)}, u32[]{:S(2)}) %copy-start) | copy-done | bytes 49176
  1.4 0.0 copy-start.2
  1.4 0.0 copy-start.1
  1.4 5.8 %product.1 = (f32[336,128]{1,0:T(8,128)S(1)}, f32[336,128]{1,0:T(8,128)S(1)}, f32[336,128]{1,0:T(8,128)S(1)}, f32[336,128]{1,0:T(8,128)S(1)}) custom-call(bf16[24,1024]{1,0:T(8,128)(2,1)S(1)} %copy-done, bf16[1024,7168]{1,0:T(8,128)(2,1)} %w_ref.1), custom_call_target="tpu_custom_call" | custom-call | flops 352321536 | bytes 14680064 | tf_op jit(solution)/shard_map/product/pallas_call | solution.py:63
  7.2 3.1 %collective-permute-start = (f32[336,128]{1,0:T(8,128)S(1)}, f32[336,128]{1,0:T(8,128)S(1)}, u32[]{:S(2)}, u32[]{:S(2)}) collective-permute-start(f32[336,128]{1,0:T(8,128)S(1)} %get-tuple-element.10), channel_id=1, source_target_pairs={{0,1},{1,0},{2,3},{3,2},{4,5},{5,4},{6,7},{7,6},{8,9},{9,8},{10,11... | collective-permute-start | bytes 516104 | tf_op jit(solution)/shard_map/ppermute | solution.py:159
  10.3 1.6 %collective-permute-start.1 = (f32[336,128]{1,0:T(8,128)S(1)}, f32[336,128]{1,0:T(8,128)S(1)}, u32[]{:S(2)}, u32[]{:S(2)}) collective-permute-start(f32[336,128]{1,0:T(8,128)S(1)} %get-tuple-element.11), channel_id=1, source_target_pairs={{0,2},{1,3},{2,0},{3,1},{4,6},{5,7},{6,4},{7,5},{8,10},{9,11},{10,... | collective-permute-start | bytes 516104 | tf_op jit(solution)/shard_map/ppermute | solution.py:159
  11.8 0.0 collective-permute-start.2
  11.9 2.8 %collective-permute-done.refs_1_ = f32[336,128]{1,0:T(8,128)S(1)} collective-permute-done((f32[336,128]{1,0:T(8,128)S(1)}, f32[336,128]{1,0:T(8,128)S(1)}, u32[]{:S(2)}, u32[]{:S(2)}) %collective-permute-start) | collective-permute-done | bytes 172064 | tf_op jit(solution)/shard_map/ppermute | solution.py:159
  14.6 2.9 %collective-permute-done.1.refs_2_ = f32[336,128]{1,0:T(8,128)S(1)} collective-permute-done((f32[336,128]{1,0:T(8,128)S(1)}, f32[336,128]{1,0:T(8,128)S(1)}, u32[]{:S(2)}, u32[]{:S(2)}) %collective-permute-start.1) | collective-permute-done | bytes 172064 | tf_op jit(solution)/shard_map/ppermute | solution.py:159
  17.5 2.1 %collective-permute-done.2.refs_3_ = f32[336,128]{1,0:T(8,128)S(1)} collective-permute-done((f32[336,128]{1,0:T(8,128)S(1)}, f32[336,128]{1,0:T(8,128)S(1)}, u32[]{:S(2)}, u32[]{:S(2)}) %collective-permute-start.2) | collective-permute-done | bytes 172064 | tf_op jit(solution)/shard_map/ppermute | solution.py:159
  19.6 2.8 %collective-permute-start.3 = (f32[168,128]{1,0:T(8,128)S(1)}, f32[168,128]{1,0:T(8,128)S(1)}, u32[]{:S(2)}, u32[]{:S(2)}) collective-permute-start(f32[168,128]{1,0:T(8,128)S(1)} %get-tuple-element.14), channel_id=1, source_target_pairs={{0,4},{1,5},{2,6},{3,7},{4,0},{5,1},{6,2},{7,3},{8,12},{9,13},{10,... | collective-permute-start | bytes 258056 | tf_op jit(solution)/shard_map/ppermute | solution.py:159
  22.4 0.0 copy-done.2
  22.5 2.6 %collective-permute-done.3.got_ref = f32[168,128]{1,0:T(8,128)S(1)} collective-permute-done((f32[168,128]{1,0:T(8,128)S(1)}, f32[168,128]{1,0:T(8,128)S(1)}, u32[]{:S(2)}, u32[]{:S(2)}) %collective-permute-start.3) | collective-permute-done | bytes 86048 | tf_op jit(solution)/shard_map/ppermute | solution.py:159
  25.1 0.0 copy-done.1
  25.1 0.9 %tail.1 = (bf16[3,7168]{1,0:T(4,128)(2,1)}, bf16[3,7168]{1,0:T(4,128)(2,1)}, f32[3,56]{1,0:T(4,128)}) custom-call(f32[168,128]{1,0:T(8,128)S(1)} %get-tuple-element.13.keep_ref, f32[168,128]{1,0:T(8,128)S(1)} %reshape.18.res_ref, f32[56,128]{1,0:T(8,128)S(1)} %bitcast.1, f32[168,128]{1,0:T(8,128)S(1)} %collective-permute-done.3.got_ref), custom_call_target="tpu_custom_call" | custom-call | tf_op jit(solution)/shard_map/tail/pallas_call | solution.py:136
  (2 shorter events, 0.1 us)
Async XLA Ops:
  0.6 0.8 %copy-start = (bf16[24,1024]{1,0:T(8,128)(2,1)S(1)}, bf16[24,1024]{1,0:T(8,128)(2,1)}, u32[]{:S(2)}) copy-start(bf16[24,1024]{1,0:T(8,128)(2,1)} %attn_hbm.1) | copy-start | bytes 147460
  1.4 21.0 %copy-start.2 = (bf16[3,7168]{1,0:T(4,128)(2,1)S(1)}, bf16[3,7168]{1,0:T(4,128)(2,1)}, u32[]{:S(2)}) copy-start(bf16[3,7168]{1,0:T(4,128)(2,1)} %param.6) | copy-start | bytes 129028
  1.4 23.7 %copy-start.1 = (f32[7168]{0:T(1024)S(1)}, f32[7168]{0:T(1024)}, u32[]{:S(2)}) copy-start(f32[7168]{0:T(1024)} %param.7) | copy-start | bytes 86020
  7.2 7.4 %collective-permute-start = (f32[336,128]{1,0:T(8,128)S(1)}, f32[336,128]{1,0:T(8,128)S(1)}, u32[]{:S(2)}, u32[]{:S(2)}) collective-permute-start(f32[336,128]{1,0:T(8,128)S(1)} %get-tuple-element.10), channel_id=1, source_target_pairs={{0,1},{1,0},{2,3},{3,2},{4,5},{5,4},{6,7},{7,6},{8,9},{9,8},{10,11... | collective-permute-start | bytes 516104 | tf_op jit(solution)/shard_map/ppermute | solution.py:159
  10.3 7.2 %collective-permute-start.1 = (f32[336,128]{1,0:T(8,128)S(1)}, f32[336,128]{1,0:T(8,128)S(1)}, u32[]{:S(2)}, u32[]{:S(2)}) collective-permute-start(f32[336,128]{1,0:T(8,128)S(1)} %get-tuple-element.11), channel_id=1, source_target_pairs={{0,2},{1,3},{2,0},{3,1},{4,6},{5,7},{6,4},{7,5},{8,10},{9,11},{10,... | collective-permute-start | bytes 516104 | tf_op jit(solution)/shard_map/ppermute | solution.py:159
  11.8 7.7 %collective-permute-start.2 = (f32[336,128]{1,0:T(8,128)S(1)}, f32[336,128]{1,0:T(8,128)S(1)}, u32[]{:S(2)}, u32[]{:S(2)}) collective-permute-start(f32[336,128]{1,0:T(8,128)S(1)} %get-tuple-element.12), channel_id=1, source_target_pairs={{0,3},{1,2},{2,1},{3,0},{4,7},{5,6},{6,5},{7,4},{8,11},{9,10},{10,... | collective-permute-start | bytes 516104 | tf_op jit(solution)/shard_map/ppermute | solution.py:159
  19.6 5.4 %collective-permute-start.3 = (f32[168,128]{1,0:T(8,128)S(1)}, f32[168,128]{1,0:T(8,128)S(1)}, u32[]{:S(2)}, u32[]{:S(2)}) collective-permute-start(f32[168,128]{1,0:T(8,128)S(1)} %get-tuple-element.14), channel_id=1, source_target_pairs={{0,4},{1,5},{2,6},{3,7},{4,0},{5,1},{6,2},{7,3},{8,12},{9,13},{10,... | collective-permute-start | bytes 258056 | tf_op jit(solution)/shard_map/ppermute | solution.py:159

commit v3 on v2

v3 whole, which is shorter than its diff:
```python
import functools
import jax
import jax.numpy as jnp
from jax import lax
from jax.experimental import pallas as pl
from jax.experimental.pallas import tpu as pltpu
from jax.sharding import PartitionSpec as P

BLOCK = 128
AXIS = "tensor"
PARTS = "dp"
MIB = 1024 * 1024
LEAD = 2
TURNS = ((0, 1, 2, 3), (0, 3, 2, 1))
STRIP = 4


def turned(near, q, odd):
    return TURNS[odd][q] if near == 4 else q


def up(value, step):
    return -(-value // step) * step


def product_kernel(near, far, rows, strips, attn_hbm, w_ref, *refs):
    outs, (attn_ref, w_buf, sems, attn_sem) = refs[:near], refs[near:]
    tokens = attn_ref.shape[0]
    held = tokens // near
    lot = up(held, 8)
    blocks = outs[0].shape[0] // held
    fetch = pltpu.make_async_copy(attn_hbm, attn_ref, attn_sem)
    fetch.start()
    spans = [pl.ds(start * BLOCK, wide * BLOCK) for start, wide in strips]
    copies = [pltpu.make_async_copy(w_ref.at[:, span], w_buf.at[:, span], sems.at[s]) for s, span in enumerate(spans)]
    for copy in copies[:LEAD]:
        copy.start()
    me = lax.axis_index(AXIS)
    pos = lax.broadcasted_iota(jnp.int32, (lot * near, tokens), 0)
    col = lax.broadcasted_iota(jnp.int32, (lot * near, tokens), 1)
    want = jnp.full_like(pos, -1)
    odd = lax.rem(lax.axis_index(PARTS), 2)
    for q in range(near):
        mask = jnp.where(odd == 1, turned(near, q, 1), turned(near, q, 0))
        for f in range(far):
            start = q * lot + f * rows
            here = (pos >= start) & (pos < start + rows)
            want = jnp.where(here, (me ^ (mask + f * near)) * rows + pos - start, want)
    pick = jnp.where(col == want, 1.0, 0.0).astype(jnp.bfloat16)
    fetch.wait()
    for copy in copies[LEAD:]:
        copy.start()
    mine = jnp.dot(pick, attn_ref[...], preferred_element_type=jnp.float32).astype(jnp.bfloat16)
    for s, (start, wide) in enumerate(strips):
        copies[s].wait()
        acc = jnp.dot(mine, w_buf[:, spans[s]], preferred_element_type=jnp.float32)
        for c in range(wide):
            for q in range(near):
                outs[q][pl.ds(start + c, held, stride=blocks), :] = acc[
                    q * lot : q * lot + held, c * BLOCK : (c + 1) * BLOCK
                ]


def cut(blocks):
    return [(start, min(STRIP, blocks - start)) for start in range(0, blocks, STRIP)]


def product(attn, w, near, rows):
    tokens, depth = attn.shape
    width = w.shape[1]
    far = tokens // (near * rows)
    strips = cut(width // BLOCK)
    part = jax.ShapeDtypeStruct((tokens // near * width // BLOCK, BLOCK), jnp.float32)
    return pl.pallas_call(
        functools.partial(product_kernel, near, far, rows, strips),
        out_shape=[part] * near,
        in_specs=[pl.BlockSpec(memory_space=pl.ANY)] * 2,
        out_specs=[pl.BlockSpec(memory_space=pltpu.VMEM)] * near,
        scratch_shapes=[
            pltpu.VMEM((tokens, depth), jnp.bfloat16),
            pltpu.VMEM((depth, width), jnp.bfloat16),
            pltpu.SemaphoreType.DMA((len(strips),)),
            pltpu.SemaphoreType.DMA,
        ],
        compiler_params=pltpu.CompilerParams(vmem_limit_bytes=40 * MIB),
        cost_estimate=pl.CostEstimate(
            flops=2 * tokens * depth * width, bytes_accessed=2 * depth * width, transcendentals=0
        ),
        name="product",
    )(pltpu.with_memory_space_constraint(attn, pltpu.HBM), pltpu.with_memory_space_constraint(w, pltpu.HBM))


def fold_kernel(*refs):
    ins, (keep_ref, send_ref) = refs[:-2], refs[-2:]
    half = keep_ref.shape[0]
    for out, start in ((keep_ref, 0), (send_ref, half)):
        lines = pl.ds(start, half)
        value = ins[0][lines, :]
        for ref in ins[1:]:
            value = value + ref[lines, :]
        out[...] = value


def fold(parts):
    half = jax.ShapeDtypeStruct((parts[0].shape[0] // 2, BLOCK), jnp.float32)
    return pl.pallas_call(
        fold_kernel,
        out_shape=[half] * 2,
        in_specs=[pl.BlockSpec(memory_space=pltpu.VMEM)] * len(parts),
        out_specs=[pl.BlockSpec(memory_space=pltpu.VMEM)] * 2,
        compiler_params=pltpu.CompilerParams(vmem_limit_bytes=12 * MIB),
        name="fold",
    )(*parts)


def tail_kernel(rows, keep_ref, res_ref, gain_ref, got_ref, new_ref, quant_ref, scale_ref, hid, nrm):
    blocks = gain_ref.shape[0]
    line = lax.broadcasted_iota(jnp.int32, (blocks, BLOCK), 0)
    lane = lax.broadcasted_iota(jnp.int32, (blocks, BLOCK), 1)
    for j in range(rows):
        at = pl.ds(j * blocks, blocks)
        hidden = keep_ref[at, :] + got_ref[at, :] + res_ref[at, :]
        hid[at, :] = hidden
        square = jnp.sum(jnp.sum(hidden * hidden, axis=0, keepdims=True), axis=1, keepdims=True)
        normed = hidden * lax.rsqrt(square / (blocks * BLOCK) + 1e-06) * gain_ref[...]
        peak = jnp.max(jnp.abs(normed), axis=1, keepdims=True) + 1e-06
        nrm[at, :] = normed * 448.0 / peak
        spread = jnp.where(line == lane, peak / 448.0, 0.0)
        scale_ref[pl.ds(j, 1), :] = jnp.sum(spread, axis=0, keepdims=True)[:, :blocks]
    for c in range(blocks):
        lanes = pl.ds(c * BLOCK, BLOCK)
        new_ref[:, lanes] = hid[pl.ds(c, rows, stride=blocks), :].astype(jnp.bfloat16)
        quant_ref[:, lanes] = nrm[pl.ds(c, rows, stride=blocks), :].astype(jnp.bfloat16)


def tail(keep, res, gain, got, rows):
    blocks = gain.shape[0]
    width = blocks * BLOCK
    return pl.pallas_call(
        functools.partial(tail_kernel, rows),
        out_shape=(
            jax.ShapeDtypeStruct((rows, width), jnp.bfloat16),
            jax.ShapeDtypeStruct((rows, width), jnp.bfloat16),
            jax.ShapeDtypeStruct((rows, blocks), jnp.float32),
        ),
        in_specs=[pl.BlockSpec(memory_space=pltpu.VMEM)] * 4,
        out_specs=[pl.BlockSpec(memory_space=pltpu.VMEM)] * 3,
        scratch_shapes=[pltpu.VMEM((rows * blocks, BLOCK), jnp.float32)] * 2,
        compiler_params=pltpu.CompilerParams(vmem_limit_bytes=8 * MIB),
        name="tail",
    )(keep, res, gain, got)


def local(attn_out, w_out, residual, norm_gain):
    groups = lax.axis_size(AXIS)
    rows, width = residual.shape
    blocks = width // BLOCK
    near = min(4, groups // 2)
    parts_of = lax.axis_size(PARTS)

    def swap(value, q):
        mask = lambda d: turned(near, q, d % 2) if q < near else q
        pairs = [(d * groups + i, d * groups + (i ^ mask(d))) for d in range(parts_of) for i in range(groups)]
        return lax.ppermute(value, (PARTS, AXIS), pairs)

    parts = product(attn_out, w_out, near, rows)
    keep, send = fold([parts[0]] + [swap(parts[q], q) for q in range(1, near)])
    mask = groups // 2
    while mask > near:
        half = keep.shape[0] // 2
        moved = swap(send, mask)
        keep, send = keep[:half] + moved[:half], keep[half:] + moved[half:]
        mask //= 2
    res = residual.astype(jnp.float32).reshape(rows * blocks, BLOCK)
    return tail(keep, res, norm_gain.reshape(blocks, BLOCK), swap(send, mask), rows)


def solution(mesh):
    step = jax.shard_map(
        local,
        mesh=mesh,
        in_specs=(P("dp", "tensor"), P("tensor", None), P(("dp", "tensor"), None), P()),
        out_specs=(P(("dp", "tensor"), None), P(("dp", "tensor"), None), P(("dp", "tensor"), None)),
        check_vma=False,
    )
    return step
```

time: 26.1 us -> 25.7 us (0.985)
  local copies, waits for them, and re-layouts: 0.83 us -> 0.04 us
  Pallas kernels: 6.68 us -> 7.23 us
    unnamed x6 -> x4, local copies, waits for them, and re-layouts: 0.8 us -> 0.01 us
    pallas_call x2, Pallas kernels: 5.81 us -> 6.36 us  [the longest x1 6.32 us: product(): pl.pallas_call(functools.partial(product_kernel, near, far, rows, strips)...]
where the time goes in v3:
time: 25.7 us; the launch traced here: 25.5 us
  waiting for transfers between devices  10.2 us (40%)
  starting transfers between devices  7.35 us (29%)
  Pallas kernels  7.23 us (28%)
  between operations  0.67 us (3%)
    ppermute x4, waiting for transfers between devices, swap(): return lax.ppermute(value, (PARTS, AXIS), pairs)  10.2 us
    ppermute x4, starting transfers between devices, swap(): return lax.ppermute(value, (PARTS, AXIS), pairs)  7.35 us
    pallas_call x1, Pallas kernels, product(): pl.pallas_call(functools.partial(product_kernel, near, far, rows, strips)...  6.32 us
    pallas_call x1, Pallas kernels, tail(): pl.pallas_call(functools.partial(tail_kernel, rows), out_shape=(jax.Shape...  0.87 us
  transfers between devices with their start and end apart: 4, of which 4 were waited for; matrix products, arithmetic and copies ran while one was open for 0% of the time, Pallas kernels for 0%

profile of v3, /device:TPU:0, one launch (start us, length us, event | category | flops | bytes accessed | tf_op | source)
XLA Modules:
  0.0 25.5 jit_solution(2632482962982109781)
XLA Ops:
  0.6 0.0 copy-start.1
  0.6 0.0 copy-start
  0.7 6.3 %product.1 = (f32[336,128]{1,0:T(8,128)S(1)}, f32[336,128]{1,0:T(8,128)S(1)}, f32[336,128]{1,0:T(8,128)S(1)}, f32[336,128]{1,0:T(8,128)S(1)}) custom-call(bf16[24,1024]{1,0:T(8,128)(2,1)} %attn_hbm.1, bf16[1024,7168]{1,0:T(8,128)(2,1)} %w_ref.1), custom_call_target="tpu_custom_call" | custom-call | flops 352321536 | bytes 14680064 | tf_op jit(solution)/shard_map/product/pallas_call | solution.py:74
  7.0 3.1 %collective-permute-start = (f32[336,128]{1,0:T(8,128)S(1)}, f32[336,128]{1,0:T(8,128)S(1)}, u32[]{:S(2)}, u32[]{:S(2)}) collective-permute-start(f32[336,128]{1,0:T(8,128)S(1)} %get-tuple-element.10), channel_id=1, source_target_pairs={{0,1},{1,0},{2,3},{3,2},{4,5},{5,4},{6,7},{7,6},{8,11},{9,10},{10,... | collective-permute-start | bytes 516104 | tf_op jit(solution)/shard_map/ppermute | solution.py:164
  10.0 1.6 %collective-permute-start.1 = (f32[336,128]{1,0:T(8,128)S(1)}, f32[336,128]{1,0:T(8,128)S(1)}, u32[]{:S(2)}, u32[]{:S(2)}) collective-permute-start(f32[336,128]{1,0:T(8,128)S(1)} %get-tuple-element.11), channel_id=1, source_target_pairs={{0,2},{1,3},{2,0},{3,1},{4,6},{5,7},{6,4},{7,5},{8,10},{9,11},{10,... | collective-permute-start | bytes 516104 | tf_op jit(solution)/shard_map/ppermute | solution.py:164
  11.6 0.0 collective-permute-start.2
  11.6 5.2 %collective-permute-done.refs_1_ = f32[336,128]{1,0:T(8,128)S(1)} collective-permute-done((f32[336,128]{1,0:T(8,128)S(1)}, f32[336,128]{1,0:T(8,128)S(1)}, u32[]{:S(2)}, u32[]{:S(2)}) %collective-permute-start) | collective-permute-done | bytes 172064 | tf_op jit(solution)/shard_map/ppermute | solution.py:164
  16.8 0.5 %collective-permute-done.1.refs_2_ = f32[336,128]{1,0:T(8,128)S(1)} collective-permute-done((f32[336,128]{1,0:T(8,128)S(1)}, f32[336,128]{1,0:T(8,128)S(1)}, u32[]{:S(2)}, u32[]{:S(2)}) %collective-permute-start.1) | collective-permute-done | bytes 172064 | tf_op jit(solution)/shard_map/ppermute | solution.py:164
  17.3 1.9 %collective-permute-done.2.refs_3_ = f32[336,128]{1,0:T(8,128)S(1)} collective-permute-done((f32[336,128]{1,0:T(8,128)S(1)}, f32[336,128]{1,0:T(8,128)S(1)}, u32[]{:S(2)}, u32[]{:S(2)}) %collective-permute-start.2) | collective-permute-done | bytes 172064 | tf_op jit(solution)/shard_map/ppermute | solution.py:164
  19.2 2.7 %collective-permute-start.3 = (f32[168,128]{1,0:T(8,128)S(1)}, f32[168,128]{1,0:T(8,128)S(1)}, u32[]{:S(2)}, u32[]{:S(2)}) collective-permute-start(f32[168,128]{1,0:T(8,128)S(1)} %get-tuple-element.14), channel_id=1, source_target_pairs={{0,4},{1,5},{2,6},{3,7},{4,0},{5,1},{6,2},{7,3},{8,12},{9,13},{10,... | collective-permute-start | bytes 258056 | tf_op jit(solution)/shard_map/ppermute | solution.py:164
  21.9 0.0 copy-done.1
  22.0 2.7 %collective-permute-done.3.got_ref = f32[168,128]{1,0:T(8,128)S(1)} collective-permute-done((f32[168,128]{1,0:T(8,128)S(1)}, f32[168,128]{1,0:T(8,128)S(1)}, u32[]{:S(2)}, u32[]{:S(2)}) %collective-permute-start.3) | collective-permute-done | bytes 86048 | tf_op jit(solution)/shard_map/ppermute | solution.py:164
  24.6 0.0 copy-done
  24.7 0.9 %tail.1 = (bf16[3,7168]{1,0:T(4,128)(2,1)}, bf16[3,7168]{1,0:T(4,128)(2,1)}, f32[3,56]{1,0:T(4,128)}) custom-call(f32[168,128]{1,0:T(8,128)S(1)} %get-tuple-element.13.keep_ref, f32[168,128]{1,0:T(8,128)S(1)} %reshape.18.res_ref, f32[56,128]{1,0:T(8,128)S(1)} %bitcast.1, f32[168,128]{1,0:T(8,128)S(1)} %collective-permute-done.3.got_ref), custom_call_target="tpu_custom_call" | custom-call | tf_op jit(solution)/shard_map/tail/pallas_call | solution.py:139
  (2 shorter events, 0.1 us)
Async XLA Ops:
  0.6 21.3 %copy-start.1 = (bf16[3,7168]{1,0:T(4,128)(2,1)S(1)}, bf16[3,7168]{1,0:T(4,128)(2,1)}, u32[]{:S(2)}) copy-start(bf16[3,7168]{1,0:T(4,128)(2,1)} %param.6) | copy-start | bytes 129028
  0.6 24.0 %copy-start = (f32[7168]{0:T(1024)S(1)}, f32[7168]{0:T(1024)}, u32[]{:S(2)}) copy-start(f32[7168]{0:T(1024)} %param.7) | copy-start | bytes 86020
  7.0 9.8 %collective-permute-start = (f32[336,128]{1,0:T(8,128)S(1)}, f32[336,128]{1,0:T(8,128)S(1)}, u32[]{:S(2)}, u32[]{:S(2)}) collective-permute-start(f32[336,128]{1,0:T(8,128)S(1)} %get-tuple-element.10), channel_id=1, source_target_pairs={{0,1},{1,0},{2,3},{3,2},{4,5},{5,4},{6,7},{7,6},{8,11},{9,10},{10,... | collective-permute-start | bytes 516104 | tf_op jit(solution)/shard_map/ppermute | solution.py:164
  10.0 7.2 %collective-permute-start.1 = (f32[336,128]{1,0:T(8,128)S(1)}, f32[336,128]{1,0:T(8,128)S(1)}, u32[]{:S(2)}, u32[]{:S(2)}) collective-permute-start(f32[336,128]{1,0:T(8,128)S(1)} %get-tuple-element.11), channel_id=1, source_target_pairs={{0,2},{1,3},{2,0},{3,1},{4,6},{5,7},{6,4},{7,5},{8,10},{9,11},{10,... | collective-permute-start | bytes 516104 | tf_op jit(solution)/shard_map/ppermute | solution.py:164
  11.6 7.5 %collective-permute-start.2 = (f32[336,128]{1,0:T(8,128)S(1)}, f32[336,128]{1,0:T(8,128)S(1)}, u32[]{:S(2)}, u32[]{:S(2)}) collective-permute-start(f32[336,128]{1,0:T(8,128)S(1)} %get-tuple-element.12), channel_id=1, source_target_pairs={{0,3},{1,2},{2,1},{3,0},{4,7},{5,6},{6,5},{7,4},{8,9},{9,8},{10,11... | collective-permute-start | bytes 516104 | tf_op jit(solution)/shard_map/ppermute | solution.py:164
  19.2 5.4 %collective-permute-start.3 = (f32[168,128]{1,0:T(8,128)S(1)}, f32[168,128]{1,0:T(8,128)S(1)}, u32[]{:S(2)}, u32[]{:S(2)}) collective-permute-start(f32[168,128]{1,0:T(8,128)S(1)} %get-tuple-element.14), channel_id=1, source_target_pairs={{0,4},{1,5},{2,6},{3,7},{4,0},{5,1},{6,2},{7,3},{8,12},{9,13},{10,... | collective-permute-start | bytes 258056 | tf_op jit(solution)/shard_map/ppermute | solution.py:164
